TPU v7x, 32 devices: a whole 2x2x4 slice. The times are simulated.
32 devices in a mesh: samp: 8 (over z, core), var: 4 (over y, x).
Axes of the slice: x: 2, y: 2, z: 4, core: 2. Of those that a mesh axis runs over, the one named last changes fastest.
Arguments:
- hap_words: int32 [2, 512, 512], P(None, 'samp', 'var'), may hold values from 0 to 1073741823
- total_counts: int32 [15360, 8192], P('samp', 'var'), may hold values from 0 to 4999
- allele_one: int32 [15360, 8192], P('samp', 'var'), may hold values from 0 to 299
- allele_two: int32 [15360, 8192], P('samp', 'var'), may hold values from 0 to 299
Outputs:
- z_total: float32 [512, 8192], P('samp', 'var')
- z_allelic: float32 [512, 8192], P('samp', 'var')
Inputs may be any that keep to these rules, and one draw needn't show every extreme that they name: Bit k, for k below 30, of hap_words[c, j, v] is haplotype c of sample 30 * j + k at variant v; higher bits are zero.
All inputs are finite; a program needn't handle non-finite values.
Results may differ from a plain program's by a relative error of at most 0.0003.
The roundings to bfloat16 on the way count: a program that leaves them out, or rounds other values in their place, can miss the bound.
Values sent between devices are 32-bit elements; how exact they have to be, the bound alone decides.
A program may use at most 192 MiB of HBM per device.

v0:
```python
import jax
import jax.numpy as jnp
from jax import lax
from jax.sharding import PartitionSpec as P

BITS = 30


def unpack(packed):
    shifts = jnp.arange(BITS, dtype=jnp.int32)
    bit_table = jnp.bitwise_and(
        jnp.right_shift(packed[:, :, None, :], shifts[None, None, :, None]), 1
    )
    return bit_table.reshape(2, packed.shape[1] * BITS, packed.shape[2])


def features(total_part, one_part, two_part):
    log_total = jnp.log1p(total_part.astype(jnp.float32))
    one_plus = one_part.astype(jnp.float32) + 1.0
    two_plus = two_part.astype(jnp.float32) + 1.0
    log_ratio = jnp.log(one_plus / two_plus)
    weight = 1.0 / (1.0 / one_plus + 1.0 / two_plus)
    return (log_total, (weight * log_ratio).astype(jnp.bfloat16), weight.astype(jnp.bfloat16))


def finish(pair_sums, dos_margin, gene_margin, sample_count):
    dos_sum, dos_sq = (dos_margin[0], dos_margin[1])
    gene_sum, gene_sq = (gene_margin[0], gene_margin[1])
    dosage_var = dos_sq - dos_sum * dos_sum / sample_count
    gene_var = gene_sq - gene_sum * gene_sum / sample_count
    covariance = pair_sums[0] - dos_sum[:, None] * gene_sum[None, :] / sample_count
    z_total = (
        jnp.sqrt(sample_count)
        * covariance
        / jnp.sqrt((dosage_var[:, None] + 1.0) * (gene_var[None, :] + 1.0))
    )
    z_allelic = pair_sums[1] / jnp.sqrt(pair_sums[2] + 1.0)
    return (z_total, z_allelic)


def per_device(hap_words, total_counts, allele_one, allele_two):
    panel_words = lax.all_gather(hap_words, "var", axis=2, tiled=True)
    bit_table = unpack(panel_words)
    dosage_b = (bit_table[0] + bit_table[1] - 1).astype(jnp.bfloat16)
    phase_int = bit_table[0] - bit_table[1]
    phase_b = phase_int.astype(jnp.bfloat16)
    phase_sq_b = (phase_int * phase_int).astype(jnp.bfloat16)
    dos_margin = jnp.stack(
        [
            jnp.sum(dosage_b, axis=0, dtype=jnp.float32),
            jnp.sum(dosage_b * dosage_b, axis=0, dtype=jnp.float32),
        ]
    )
    log_total, weighted_b, weight_b = features(total_counts, allele_one, allele_two)
    gene_margin = jnp.stack([jnp.sum(log_total, axis=0), jnp.sum(log_total * log_total, axis=0)])
    cross_total = jnp.einsum(
        "sv,sg->vg", dosage_b, log_total.astype(jnp.bfloat16), preferred_element_type=jnp.float32
    )
    cross_allelic = jnp.einsum("sv,sg->vg", phase_b, weighted_b, preferred_element_type=jnp.float32)
    het_weight = jnp.einsum("sv,sg->vg", phase_sq_b, weight_b, preferred_element_type=jnp.float32)
    pair_sums = jnp.stack([cross_total, cross_allelic, het_weight])
    sample_groups = lax.axis_size("samp")
    sample_count = jnp.float32(bit_table.shape[1] * sample_groups)
    own_pairs, own_dos = (
        lax.psum_scatter(pair_sums, "samp", scatter_dimension=1, tiled=True),
        lax.psum_scatter(dos_margin, "samp", scatter_dimension=1, tiled=True),
    )
    summed_genes = lax.psum(gene_margin, "samp")
    return finish(own_pairs, own_dos, summed_genes, sample_count)


def solution(mesh):
    in_specs = (P(None, "samp", "var"), P("samp", "var"), P("samp", "var"), P("samp", "var"))
    out_specs = (P("samp", "var"), P("samp", "var"))
    return jax.shard_map(
        per_device, mesh=mesh, in_specs=in_specs, out_specs=out_specs, check_vma=False
    )
```

profile of v0, /device:TPU:0, one launch (start us, length us, event | category | flops | bytes accessed | tf_op | source)
XLA Modules:
  0.0 234.2 jit_solution(2295800869853956210)
XLA Ops:
  7.2 0.0 reduce-scatter.7.cloned.1.call-start
  7.2 11.8 %all_gather.3 = s32[2,64,512]{2,1,0:T(8,128)S(1)} all-gather(s32[2,64,128]{2,1,0:T(8,128)} %param.4), channel_id=1, replica_groups=mesh['samp'=8,'var'=4] {'var'}, dimensions={2}, use_global_device_ids=true | all-gather | bytes 327680 | tf_op jit(solution)/shard_map/all_gather | solution.py:42
  19.0 1.3 shift-right-arithmetic_and_fusion
  20.3 0.0 copy-start
  20.3 3.2 %copy-done = s32[2,64,30,512]{3,2,1,0:T(8,128)} copy-done((s32[2,64,30,512]{3,2,1,0:T(8,128)}, s32[2,64,30,512]{3,2,1,0:T(8,128)S(1)}, u32[]{:S(2)}) %copy-start) | copy-done | bytes 7864344
  23.5 1.4 convert_reduce_fusion.1
  24.9 0.9 copy.6
  25.8 0.0 reduce-scatter.7.cloned.1.call-update
  25.8 0.2 reduce-scatter.5.cloned.1.call-start
  26.0 6.9 %fusion.14 = (bf16[1,64,30,512]{3,2,1,0:T(8,128)(2,1)}, bf16[1,64,30,512]{3,2,1,0:T(8,128)(2,1)}) fusion(s32[2,64,30,512]{3,2,1,0:T(8,128)} %copy-done), kind=kLoop, calls=%fused_computation.22 | loop fusion | flops 3932160 | bytes 11796480 | tf_op jit(solution)/shard_map/convert_element_type | solution.py:46
  32.9 1.5 convert_element_type.47
  34.4 2.6 %convert_element_type.51 = bf16[1920,512]{1,0:T(8,128)(2,1)S(1)} reshape(bf16[1,64,30,512]{3,2,1,0:T(8,128)(2,1)} %get-tuple-element.7) | data formatting | bytes 3932160 | tf_op jit(solution)/shard_map/convert_element_type | solution.py:46
  37.0 3.9 %convert_element_type.56 = bf16[1920,512]{1,0:T(8,128)(2,1)} reshape(bf16[1,64,30,512]{3,2,1,0:T(8,128)(2,1)} %get-tuple-element.8) | data formatting | bytes 3932160 | tf_op jit(solution)/shard_map/convert_element_type | solution.py:47
  40.9 0.0 copy-start.2
  40.9 14.6 %fusion.7 = f32[1,512,2048]{2,1,0:T(8,128)S(1)} fusion(bf16[1920,512]{1,0:T(8,128)(2,1)S(1)} %convert_element_type.51, s32[1920,2048]{1,0:T(8,128)} %param.6, s32[1920,2048]{1,0:T(8,128)} %param.7), kind=kOutput, calls=%fused_computation.19 | convolution fusion | flops 4069785600 | bytes 37617664 | tf_op jit(solution)/shard_map/sv,sg->vg/dot_general | solution.py:59
  55.5 0.0 copy-done.2
  55.5 0.0 copy-start.1
  55.5 15.1 %fusion.8 = f32[1,512,2048]{2,1,0:T(8,128)} fusion(bf16[1920,512]{1,0:T(8,128)(2,1)S(1)} %copy-done.2, s32[1920,2048]{1,0:T(8,128)} %param.6, s32[1920,2048]{1,0:T(8,128)} %param.7), kind=kOutput, calls=%fused_computation.20 | convolution fusion | flops 4061921280 | bytes 37617664 | tf_op jit(solution)/shard_map/sv,sg->vg/dot_general | solution.py:60
  70.7 0.0 copy-done.1
  70.7 12.8 %fusion.11 = f32[1,512,2048]{2,1,0:T(8,128)} fusion(bf16[1920,512]{1,0:T(8,128)(2,1)S(1)} %copy-done.1, s32[1920,2048]{1,0:T(8,128)} %param.5), kind=kOutput, calls=%fused_computation.21 | convolution fusion | flops 4034396160 | bytes 21889024 | tf_op jit(solution)/shard_map/sv,sg->vg/dot_general | solution.py:56
  83.5 9.9 %pad_maximum_fusion = f32[3,512,2048]{2,1,0:T(8,128)} fusion(f32[1,512,2048]{2,1,0:T(8,128)} %fusion.8, f32[1,512,2048]{2,1,0:T(8,128)S(1)} %fusion.7, f32[1,512,2048]{2,1,0:T(8,128)} %fusion.11), kind=kLoop, calls=%fused_computation.8 | loop fusion | flops 6291456 | bytes 25165824 | tf_op jit(solution)/shard_map/stack | solution.py:61
  93.4 0.0 reduce-scatter.5.cloned.1.call-update
  93.4 12.1 %fusion = (f32[2048]{0:T(1024)S(1)}, f32[2048]{0:T(1024)S(1)}) fusion(s32[1920,2048]{1,0:T(8,128)} %param.5), kind=kLoop, calls=%fused_computation.6 | loop fusion | flops 15724544 | bytes 15745024 | tf_op jit(solution)/shard_map/reduce_sum | solution.py:55
  105.5 28.7 %psum.7 = f32[2,2048]{1,0:T(2,128)S(1)} all-reduce(f32[2,2048]{1,0:T(2,128)S(1)} %pad_maximum_fusion.1), channel_id=1, replica_groups=mesh['samp'=8,'var'=4] {'samp'}, use_global_device_ids=true, to_apply=%region_6.0 | all-reduce | flops 4096 | bytes 32768 | tf_op jit(solution)/shard_map/psum | solution.py:68
  134.2 0.0 reduce-scatter.7.cloned.1.call-done
  134.2 0.9 fusion.24
  135.2 0.1 copy.8
  135.2 0.1 copy.9
  135.3 87.9 %reduce-scatter.5.cloned.1.call-done = f32[3,64,2048]{2,1,0:T(8,128)} async-done(((f32[3,512,2048]{2,1,0:T(8,128)}), f32[3,64,2048]{2,1,0:T(8,128)}) %reduce-scatter.5.cloned.1.call-update) | async-done | bytes 1572880 | tf_op jit(solution)/shard_map/reduce_scatter | solution.py:65
  223.2 2.1 fusion.17
  225.3 2.0 fusion.20
  (4 shorter events, 0.1 us)
Async XLA Ops:
  7.2 127.1 %reduce-scatter.7.cloned.1.call-start = ((), (), s32[]{:S(2)}) async-start(), calls=%async_computation.3 | async-start | bytes 294912
  20.3 3.2 %copy-start = (s32[2,64,30,512]{3,2,1,0:T(8,128)}, s32[2,64,30,512]{3,2,1,0:T(8,128)S(1)}, u32[]{:S(2)}) copy-start(s32[2,64,30,512]{3,2,1,0:T(8,128)S(1)} %shift-right-arithmetic_and_fusion) | copy-start | bytes 23592964
  25.8 197.5 %reduce-scatter.5.cloned.1.call-start = ((), (), s32[]{:S(2)}) async-start(), calls=%async_computation.2 | async-start | bytes 14155776 | tf_op jit(solution)/shard_map/reduce_scatter | solution.py:65
  40.9 14.6 %copy-start.2 = (bf16[1920,512]{1,0:T(8,128)(2,1)S(1)}, bf16[1920,512]{1,0:T(8,128)(2,1)}, u32[]{:S(2)}) copy-start(bf16[1920,512]{1,0:T(8,128)(2,1)} %convert_element_type.56) | copy-start | bytes 5898244
  55.5 15.2 %copy-start.1 = (bf16[1920,512]{1,0:T(8,128)(2,1)S(1)}, bf16[1920,512]{1,0:T(8,128)(2,1)}, u32[]{:S(2)}) copy-start(bf16[1920,512]{1,0:T(8,128)(2,1)} %convert_element_type.47) | copy-start | bytes 5898244
Sparse Core Ops, SparseCore 0:
  25.9 30.7 reduce-scatter.6
  93.5 129.7 reduce-scatter.4
where the time goes:
time: 235 us; the launch traced here: 234 us
  waiting for transfers between devices  88 us (37%)
  matrix products  42.6 us (18%)
  blocking collectives  40.5 us (17%)
  other arithmetic  35.6 us (15%)
  between operations  14.1 us (6%)
  local copies, waits for them, and re-layouts  13.1 us (6%)
    reduce_scatter x1, waiting for transfers between devices, per_device(): lax.psum_scatter(pair_sums, 'samp', scatter_dimension=1, tiled=True)  87.9 us
    psum x1, blocking collectives, per_device(): summed_genes = lax.psum(gene_margin, 'samp')  28.7 us
    dot_general x1, matrix products, per_device(): jnp.einsum('sv,sg->vg', phase_sq_b, weight_b, preferred_element_type=jnp....  15.1 us
    dot_general x1, matrix products, per_device(): jnp.einsum('sv,sg->vg', phase_b, weighted_b, preferred_element_type=jnp.f...  14.6 us
    dot_general x1, matrix products, per_device(): jnp.einsum('sv,sg->vg', dosage_b, log_total.astype(jnp.bfloat16), preferr...  12.8 us
    reduce_sum x1, other arithmetic, per_device(): jnp.sum(log_total, axis=0)  12.1 us
    all_gather x1, blocking collectives, per_device(): panel_words = lax.all_gather(hap_words, 'var', axis=2, tiled=True)  11.8 us
    another operation x1, other arithmetic, per_device(): pair_sums = jnp.stack([cross_total, cross_allelic, het_weight])  9.86 us
  transfers between devices with their start and end apart: 2, of which 1 were waited for; matrix products, arithmetic and copies ran while one was open for 34% of the time, Pallas kernels for 0%

commit v1 on v0

--- a/solution.py
+++ b/solution.py
@@ -4,6 +4,14 @@
 from jax.sharding import PartitionSpec as P
 
 BITS = 30
+
+
+def added_up(x, mesh_axis):
+    count, total = (lax.axis_size(mesh_axis), x)
+    for far in [1 << k for k in range(count.bit_length() - 1)]:
+        route = [(i, i ^ far) for i in range(count)]
+        total = total + lax.ppermute(total, mesh_axis, route)
+    return total
 
 
 def unpack(packed):
@@ -65,7 +73,7 @@
         lax.psum_scatter(pair_sums, "samp", scatter_dimension=1, tiled=True),
         lax.psum_scatter(dos_margin, "samp", scatter_dimension=1, tiled=True),
     )
-    summed_genes = lax.psum(gene_margin, "samp")
+    summed_genes = added_up(gene_margin, "samp")
     return finish(own_pairs, own_dos, summed_genes, sample_count)
 
 

time: 235 us -> 241 us (1.026)
  blocking collectives: 40.5 us -> 11.8 us
  waiting for transfers between devices: 88 us -> 112 us
  matrix products: 42.6 us -> 47.5 us
  starting transfers between devices: 0.26 us -> 4.57 us
    psum x1 -> x0, blocking collectives: 28.7 us -> none  [per_device(): summed_genes = lax.psum(gene_margin, 'samp')]
    reduce_scatter x1, waiting for transfers between devices: 87.9 us -> 107 us  [per_device(): lax.psum_scatter(pair_sums, 'samp', scatter_dimension=1, tiled=True)]
    ppermute x0 -> x3, waiting for transfers between devices: none -> 5.57 us  [added_up(): total = total + lax.ppermute(total, mesh_axis, route)]
    ppermute x0 -> x3, starting transfers between devices: none -> 4.31 us  [added_up(): total = total + lax.ppermute(total, mesh_axis, route)]
    dot_general x1, matrix products: 12.8 us -> 15.3 us  [per_device(): jnp.einsum('sv,sg->vg', dosage_b, log_total.astype(jnp.bfloat16), preferr...]
  transfers between devices with their start and end apart: 2 -> 5, of which waited for: 1 -> 4; matrix products, arithmetic and copies ran while one was open for 34% -> 36% of each run, Pallas kernels for 0% -> 0%
where the time goes in v1:
time: 241 us; the launch traced here: 240 us
  waiting for transfers between devices  112 us (46%)
  matrix products  47.5 us (20%)
  other arithmetic  35.8 us (15%)
  local copies, waits for them, and re-layouts  14.4 us (6%)
  between operations  14.1 us (6%)
  blocking collectives  11.8 us (5%)
  starting transfers between devices  4.57 us (2%)
    reduce_scatter x1, waiting for transfers between devices, per_device(): lax.psum_scatter(pair_sums, 'samp', scatter_dimension=1, tiled=True)  107 us
    dot_general x1, matrix products, per_device(): jnp.einsum('sv,sg->vg', phase_b, weighted_b, preferred_element_type=jnp.f...  16.4 us
    dot_general x1, matrix products, per_device(): jnp.einsum('sv,sg->vg', phase_sq_b, weight_b, preferred_element_type=jnp....  15.8 us
    dot_general x1, matrix products, per_device(): jnp.einsum('sv,sg->vg', dosage_b, log_total.astype(jnp.bfloat16), preferr...  15.3 us
    reduce_sum x1, other arithmetic, per_device(): jnp.sum(log_total, axis=0)  12.3 us
    all_gather x1, blocking collectives, per_device(): panel_words = lax.all_gather(hap_words, 'var', axis=2, tiled=True)  11.8 us
    another operation x1, other arithmetic, per_device(): pair_sums = jnp.stack([cross_total, cross_allelic, het_weight])  9.86 us
    convert_element_type x1, other arithmetic, per_device(): phase_b = phase_int.astype(jnp.bfloat16)  6.77 us
  transfers between devices with their start and end apart: 5, of which 4 were waited for; matrix products, arithmetic and copies ran while one was open for 36% of the time, Pallas kernels for 0%

profile of v1, /device:TPU:0, one launch (start us, length us, event | category | flops | bytes accessed | tf_op | source)
XLA Modules:
  0.0 240.4 jit_solution(15230521868294346213)
XLA Ops:
  7.2 0.0 reduce-scatter.7.cloned.1.call-start
  7.2 11.8 %all_gather.3 = s32[2,64,512]{2,1,0:T(8,128)S(1)} all-gather(s32[2,64,128]{2,1,0:T(8,128)} %param.4), channel_id=1, replica_groups=mesh['samp'=8,'var'=4] {'var'}, dimensions={2}, use_global_device_ids=true | all-gather | bytes 327680 | tf_op jit(solution)/shard_map/all_gather | solution.py:50
  19.0 1.3 shift-right-arithmetic_and_fusion
  20.3 0.0 copy-start
  20.3 3.2 %copy-done = s32[2,64,30,512]{3,2,1,0:T(8,128)} copy-done((s32[2,64,30,512]{3,2,1,0:T(8,128)}, s32[2,64,30,512]{3,2,1,0:T(8,128)S(1)}, u32[]{:S(2)}) %copy-start) | copy-done | bytes 7864344
  23.5 1.4 convert_reduce_fusion.1
  24.9 0.9 copy.6
  25.8 0.0 reduce-scatter.7.cloned.1.call-update
  25.8 0.2 reduce-scatter.5.cloned.1.call-start
  26.0 6.8 %fusion.14 = (bf16[1,64,30,512]{3,2,1,0:T(8,128)(2,1)}, bf16[1,64,30,512]{3,2,1,0:T(8,128)(2,1)}) fusion(s32[2,64,30,512]{3,2,1,0:T(8,128)} %copy-done), kind=kLoop, calls=%fused_computation.22 | loop fusion | flops 3932160 | bytes 11796480 | tf_op jit(solution)/shard_map/convert_element_type | solution.py:54
  32.8 3.9 %convert_element_type.56 = bf16[1920,512]{1,0:T(8,128)(2,1)} reshape(bf16[1,64,30,512]{3,2,1,0:T(8,128)(2,1)} %get-tuple-element.8) | data formatting | bytes 3932160 | tf_op jit(solution)/shard_map/convert_element_type | solution.py:55
  36.7 3.8 %convert_element_type.51 = bf16[1920,512]{1,0:T(8,128)(2,1)} reshape(bf16[1,64,30,512]{3,2,1,0:T(8,128)(2,1)} %get-tuple-element.7) | data formatting | bytes 3932160 | tf_op jit(solution)/shard_map/convert_element_type | solution.py:54
  40.5 15.8 %fusion.8 = f32[1,512,2048]{2,1,0:T(8,128)} fusion(bf16[1920,512]{1,0:T(8,128)(2,1)} %convert_element_type.56, s32[1920,2048]{1,0:T(8,128)} %param.6, s32[1920,2048]{1,0:T(8,128)} %param.7), kind=kOutput, calls=%fused_computation.20 | convolution fusion | flops 4061921280 | bytes 37617664 | tf_op jit(solution)/shard_map/sv,sg->vg/dot_general | solution.py:68
  56.3 16.4 %fusion.7 = f32[1,512,2048]{2,1,0:T(8,128)} fusion(bf16[1920,512]{1,0:T(8,128)(2,1)S(1)} %copy-done.2, s32[1920,2048]{1,0:T(8,128)} %param.6, s32[1920,2048]{1,0:T(8,128)} %param.7), kind=kOutput, calls=%fused_computation.19 | convolution fusion | flops 4069785600 | bytes 37617664 | tf_op jit(solution)/shard_map/sv,sg->vg/dot_general | solution.py:67
  72.7 1.6 convert_element_type.47
  74.3 15.3 %fusion.11 = f32[1,512,2048]{2,1,0:T(8,128)} fusion(bf16[1920,512]{1,0:T(8,128)(2,1)} %convert_element_type.47, s32[1920,2048]{1,0:T(8,128)} %param.5), kind=kOutput, calls=%fused_computation.21 | convolution fusion | flops 4034396160 | bytes 21889024 | tf_op jit(solution)/shard_map/sv,sg->vg/dot_general | solution.py:64
  89.6 0.0 copy-done.1
  89.6 9.9 %pad_maximum_fusion = f32[3,512,2048]{2,1,0:T(8,128)} fusion(f32[1,512,2048]{2,1,0:T(8,128)S(1)} %copy-done.1, f32[1,512,2048]{2,1,0:T(8,128)} %fusion.7, f32[1,512,2048]{2,1,0:T(8,128)} %fusion.11), kind=kLoop, calls=%fused_computation.8 | loop fusion | flops 6291456 | bytes 25165824 | tf_op jit(solution)/shard_map/stack | solution.py:69
  99.5 0.0 reduce-scatter.5.cloned.1.call-update
  99.5 12.3 %fusion = (f32[2048]{0:T(1024)S(1)}, f32[2048]{0:T(1024)S(1)}) fusion(s32[1920,2048]{1,0:T(8,128)} %param.5), kind=kLoop, calls=%fused_computation.6 | loop fusion | flops 15724544 | bytes 15745024 | tf_op jit(solution)/shard_map/reduce_sum | solution.py:63
  111.9 0.1 collective-permute-start
  111.9 1.2 collective-permute-done
  113.1 1.6 collective-permute-start.1
  114.8 0.9 fusion.25
  115.7 0.1 copy.9
  115.8 0.1 copy.8
  115.8 1.7 collective-permute-done.1
  117.5 2.6 %collective-permute-start.2 = (f32[2,2048]{1,0:T(2,128)S(1)}, f32[2,2048]{1,0:T(2,128)S(1)}, u32[]{:S(2)}, u32[]{:S(2)}) collective-permute-start(f32[2,2048]{1,0:T(2,128)S(1)} %fusion.30), channel_id=1, source_target_pairs={{0,16},{4,20},{8,24},{12,28},{16,0},{20,4},{24,8},{28,12},{1,17},{... | collective-permute-start | bytes 49160 | tf_op jit(solution)/shard_map/ppermute | solution.py:13
  120.1 2.7 %collective-permute-done.2 = f32[2,2048]{1,0:T(2,128)S(1)} collective-permute-done((f32[2,2048]{1,0:T(2,128)S(1)}, f32[2,2048]{1,0:T(2,128)S(1)}, u32[]{:S(2)}, u32[]{:S(2)}) %collective-permute-start.2) | collective-permute-done | bytes 16416 | tf_op jit(solution)/shard_map/ppermute | solution.py:13
  122.9 106.6 %reduce-scatter.5.cloned.1.call-done = f32[3,64,2048]{2,1,0:T(8,128)} async-done(((f32[3,512,2048]{2,1,0:T(8,128)}), f32[3,64,2048]{2,1,0:T(8,128)}) %reduce-scatter.5.cloned.1.call-update) | async-done | bytes 1572880 | tf_op jit(solution)/shard_map/reduce_scatter | solution.py:73
  229.5 2.1 fusion.17
  231.5 2.0 fusion.20
  (11 shorter events, 0.1 us)
Async XLA Ops:
  7.2 107.6 %reduce-scatter.7.cloned.1.call-start = ((), (), s32[]{:S(2)}) async-start(), calls=%async_computation.3 | async-start | bytes 294912
  20.3 3.2 %copy-start = (s32[2,64,30,512]{3,2,1,0:T(8,128)}, s32[2,64,30,512]{3,2,1,0:T(8,128)S(1)}, u32[]{:S(2)}) copy-start(s32[2,64,30,512]{3,2,1,0:T(8,128)S(1)} %shift-right-arithmetic_and_fusion) | copy-start | bytes 23592964
  25.8 203.7 %reduce-scatter.5.cloned.1.call-start = ((), (), s32[]{:S(2)}) async-start(), calls=%async_computation.2 | async-start | bytes 14155776 | tf_op jit(solution)/shard_map/reduce_scatter | solution.py:73
  40.5 15.8 %copy-start.2 = (bf16[1920,512]{1,0:T(8,128)(2,1)S(1)}, bf16[1920,512]{1,0:T(8,128)(2,1)}, u32[]{:S(2)}) copy-start(bf16[1920,512]{1,0:T(8,128)(2,1)} %convert_element_type.51) | copy-start | bytes 5898244
  74.3 15.3 %copy-start.1 = (f32[1,512,2048]{2,1,0:T(8,128)S(1)}, f32[1,512,2048]{2,1,0:T(8,128)}, u32[]{:S(2)}) copy-start(f32[1,512,2048]{2,1,0:T(8,128)} %fusion.8) | copy-start | bytes 12582916
  111.9 1.2 collective-permute-start
  113.1 4.3 %collective-permute-start.1 = (f32[2,2048]{1,0:T(2,128)S(1)}, f32[2,2048]{1,0:T(2,128)S(1)}, u32[]{:S(2)}, u32[]{:S(2)}) collective-permute-start(f32[2,2048]{1,0:T(2,128)S(1)} %fusion.24), channel_id=1, source_target_pairs={{0,8},{4,12},{8,0},{12,4},{16,24},{20,28},{24,16},{28,20},{1,9},{5... | collective-permute-start | bytes 49160 | tf_op jit(solution)/shard_map/ppermute | solution.py:13
  117.5 5.4 %collective-permute-start.2 = (f32[2,2048]{1,0:T(2,128)S(1)}, f32[2,2048]{1,0:T(2,128)S(1)}, u32[]{:S(2)}, u32[]{:S(2)}) collective-permute-start(f32[2,2048]{1,0:T(2,128)S(1)} %fusion.30), channel_id=1, source_target_pairs={{0,16},{4,20},{8,24},{12,28},{16,0},{20,4},{24,8},{28,12},{1,17},{... | collective-permute-start | bytes 49160 | tf_op jit(solution)/shard_map/ppermute | solution.py:13
Sparse Core Ops, SparseCore 0:
  25.9 30.7 reduce-scatter.6
  99.6 129.8 reduce-scatter.4
